TPU v7x, 256 devices: a whole 4x4x8 slice. The times are simulated.
256 devices in a mesh: blk: 64 (over x, y_lo, z), grp: 4 (over y_hi, core).
Axes of the slice: x: 4, y: 4 (y_hi: 2, y_lo: 2; y = y_hi * 2 + y_lo), z: 8, core: 2. Of those that a mesh axis runs over, the one named last changes fastest.
Arguments:
- sources: bfloat16 [65536, 256], P('blk'), may hold values from -64 to 64
- positive: int32 [65536], P('blk'), may hold values from 0 to 65535
- src_part: int32 [65536], P('blk'), may hold values from 0 to 7
- destinations: bfloat16 [65536, 256], P(('blk', 'grp')), may hold values from -8 to 8
- dst_part: int32 [65536], P(('blk', 'grp')), may hold values from 0 to 7
Outputs:
- loss: float32 [65536], P('blk')
All inputs are finite; a program needn't handle non-finite values.
Results may differ from a plain program's by a relative error of at most 0.0003.
Values may be sent and summed in bfloat16 or wider, within the bound.
A program may use at most 192 MiB of HBM per device.

v0:
```python
import jax
import jax.numpy as jnp
from jax import lax
from jax.sharding import Mesh
from jax.sharding import PartitionSpec as P

BLK = ("blk_0", "blk_1", "blk_2")
BLK_GRP = ("blk_0", "blk_1", "blk_2", "grp")


SCALE = 3.0
NEG = -1e30


def joined_along(parts, dim):
    dims = list(parts.shape[1:])
    dims[dim] *= parts.shape[0]
    return jnp.moveaxis(parts, 0, dim).reshape(dims)


def stacked_from(x, axes, order):
    parts = x[None]
    for k in order:
        parts = lax.all_gather(parts, axes[k], axis=0, tiled=True)
    held = [lax.axis_size(axes[k]) for k in reversed(order)]
    parts = parts.reshape(*held, *x.shape)
    turned = sorted(range(len(order)), key=lambda place: order[len(order) - 1 - place])
    return parts.transpose(*turned, *range(len(order), parts.ndim)).reshape(-1, *x.shape)


def whole_of(x, axes, order, dim):
    return joined_along(stacked_from(x, axes, order), dim)


def copy_for_each(x, axis):
    size = lax.axis_size(axis)
    return lax.all_to_all(jnp.broadcast_to(x[None], (size, *x.shape)), axis, 0, 0, tiled=True)


def collected_together(x, axis):
    leaves = jax.tree.leaves(x)
    order = sorted(range(len(leaves)), key=lambda k: -leaves[k].size)
    width = (1, *leaves[order[0]].shape)[-1]
    lines = [
        jnp.pad(leaves[k].reshape(-1), (0, -leaves[k].size % width)).reshape(-1, width)
        for k in order
    ]
    both, at, found = (copy_for_each(jnp.concatenate(lines), axis), 0, {})
    for k, line in zip(order, lines):
        section = both[:, at : at + len(line)].reshape(len(both), -1)
        found[k] = section[:, : leaves[k].size].reshape(-1, *leaves[k].shape)
        at += len(line)
    numbers = iter(range(len(leaves)))
    return jax.tree.map(lambda _: found[next(numbers)], x)


def combined_pairwise(pieces, combine):
    while len(jax.tree.leaves(pieces)[0]) > 1:
        pieces = jax.vmap(combine)(
            *(jax.tree.map(lambda part: part[side::2], pieces) for side in (0, 1))
        )
    return jax.tree.map(lambda part: part[0], pieces)


def joined_all(x, axis, combine):
    pieces = collected_together(x, axis)
    return combined_pairwise(pieces, combine)


def global_columns(count, width, group, groups):
    flat = jnp.arange(count, dtype=jnp.int32)
    return flat // width * (groups * width) + group * width + flat % width


def score_block(carry, sources, positive, src_part, block, block_part, columns):
    maxima, totals, pos_logit = carry
    logits = SCALE * lax.dot_general(
        sources, block, (((1,), (1,)), ((), ())), preferred_element_type=jnp.float32
    )
    is_pos = columns[None, :] == positive[:, None]
    keep = (block_part[None, :] != src_part[:, None]) | is_pos
    masked = jnp.where(keep, logits, NEG)
    new_max = jnp.maximum(maxima, jnp.max(masked, axis=1))
    weights = jnp.where(keep, jnp.exp(masked - new_max[:, None]), 0.0)
    totals = jnp.sum(weights, axis=1)
    pos_logit = jnp.sum(jnp.where(is_pos, logits, 0.0), axis=1)
    return (new_max, totals, pos_logit)


def combine(first, second):
    max_a, sum_a, pos_a = first
    max_b, sum_b, pos_b = second
    top = jnp.maximum(max_a, max_b)
    return (top, sum_a * jnp.exp(max_a - top) + sum_b * jnp.exp(max_b - top), pos_a + pos_b)


def on_device(sources, positive, src_part, destinations, dst_part):
    width = destinations.shape[0]
    count_rows = sources.shape[0]
    groups = lax.axis_size("grp")
    group = lax.axis_index("grp")
    start = (
        jnp.full((count_rows,), NEG, jnp.float32),
        jnp.zeros((count_rows,), jnp.float32),
        jnp.zeros((count_rows,), jnp.float32),
    )
    block = whole_of(destinations, BLK, (1, 0, 2), 0)
    columns = global_columns(block.shape[0], width, group, groups)
    carry = score_block(
        start, sources, positive, src_part, block, whole_of(dst_part, BLK, (1, 0, 2), 0), columns
    )
    maxima, totals, pos_logit = joined_all(carry, "grp", combine)
    return maxima + jnp.log(totals) - pos_logit


def solution(mesh):
    finer = Mesh(
        mesh.devices.reshape(4, 2, 8, mesh.shape["grp"]), ("blk_0", "blk_1", "blk_2", "grp")
    )
    placed = (P(BLK, None), P(BLK), P(BLK), P(BLK_GRP, None), P(BLK_GRP))
    return jax.shard_map(on_device, mesh=finer, in_specs=placed, out_specs=P(BLK), check_vma=False)
```

profile of v0, /device:TPU:1, one launch (start us, length us, event | category | flops | bytes accessed | tf_op | source)
XLA Modules:
  0.0 231.4 jit_solution(11904566351215980522)
XLA Ops:
  6.5 0.0 copy-start
  6.5 0.0 all-gather.7.cloned.1.call-start
  6.5 7.1 %all-gather.1 = bf16[512,256]{1,0:T(8,128)(2,1)} all-gather(bf16[256,256]{1,0:T(8,128)(2,1)} %param.8), channel_id=3, replica_groups=mesh['blk_0'=4,'blk_1'=2,'blk_2'=8,'grp'=4] {'blk_1'}, dimensions={0}, use_global_device_ids=true | all-gather | bytes 393216 | tf_op jit(solution)/shard_map/all_gather | solution.py:24
  13.7 0.0 all-gather.7.cloned.1.call-update
  13.7 0.0 all-gather.9.cloned.1.call-start
  13.7 28.8 %all-gather.7.cloned.1.call-done = bf16[8,256,256]{2,1,0:T(8,128)(2,1)} async-done(((bf16[2,256,256]{2,1,0:T(8,128)(2,1)}), bf16[8,256,256]{2,1,0:T(8,128)(2,1)}) %all-gather.7.cloned.1.call-update) | async-done | bytes 1048592 | tf_op jit(solution)/shard_map/all_gather | solution.py:24
  42.5 0.0 all-gather.9.cloned.1.call-update
  42.5 3.3 %all-gather.2 = s32[2,1,256]{2,1,0:T(1,128)S(1)} all-gather(s32[1,1,256]{2,1,0:T(1,128)} %bitcast.35), channel_id=2, replica_groups=mesh['blk_0'=4,'blk_1'=2,'blk_2'=8,'grp'=4] {'blk_1'}, dimensions={0}, use_global_device_ids=true | all-gather | bytes 3072 | tf_op jit(solution)/shard_map/all_gather | solution.py:24
  45.8 8.1 %all-gather.3 = s32[4,2,256]{2,1,0:T(2,128)S(1)} all-gather(s32[1,2,256]{2,1,0:T(2,128)S(1)} %copy.15), channel_id=1, replica_groups=mesh['blk_0'=4,'blk_1'=2,'blk_2'=8,'grp'=4] {'blk_0'}, dimensions={0}, use_global_device_ids=true | all-gather | bytes 10240 | tf_op jit(solution)/shard_map/all_gather | solution.py:24
  54.0 22.8 %all_gather.20 = s32[64,256]{1,0:T(8,128)S(1)} all-gather(s32[8,256]{1,0:T(8,128)S(1)} %reshape.76), channel_id=1, replica_groups=mesh['blk_0'=4,'blk_1'=2,'blk_2'=8,'grp'=4] {'blk_2'}, dimensions={0}, use_global_device_ids=true | all-gather | bytes 73728 | tf_op jit(solution)/shard_map/all_gather | solution.py:24
  76.8 64.4 %all-gather.9.cloned.1.call-done = bf16[64,256,256]{2,1,0:T(8,128)(2,1)} async-done(((bf16[8,256,256]{2,1,0:T(8,128)(2,1)}), bf16[64,256,256]{2,1,0:T(8,128)(2,1)}) %all-gather.9.cloned.1.call-update) | async-done | bytes 8388624 | tf_op jit(solution)/shard_map/all_gather | solution.py:24
  141.2 7.6 %copy.17 = bf16[4,2,8,256,256]{4,3,2,1,0:T(8,128)(2,1)} copy(bf16[4,2,8,256,256]{4,3,1,0,2:T(8,128)(2,1)} %bitcast.23) | data formatting | bytes 16777216 | tf_op jit(solution)/shard_map/transpose | solution.py:28
  148.8 0.0 copy-start.1
  148.8 0.0 copy-start.2
  148.8 0.0 copy-done
  148.8 28.2 %fusion.1 = (f32[1024]{0:T(1024)S(1)}, f32[1024,16384]{1,0:T(8,128)}) fusion(s32[16384]{0:T(1024)S(1)} %fusion.10, s32[16384]{0:T(1024)S(1)} %bitcast.26, s32[1024]{0:T(1024)} %param.6, s32[1024]{0:T(1024)} %param.7, bf16[1024,256]{1,0:T(8,128)(2,1)S(1)} %copy-done, bf16[16384,256]{1,0:T(8,128)(2,1)} %bitcast.24), kind=kOutput, calls=%fused_computation.5 | convolution fusion | flops 8690596864 | bytes 76165120 | tf_op jit(solution)/shard_map/dot_general | solution.py:77
  177.0 0.0 copy-done.1
  177.0 0.0 copy-done.2
  177.0 36.9 %select_reduce_fusion = (f32[1024]{0:T(1024)S(1)}, f32[1024]{0:T(1024)S(1)}) fusion(f32[1024,16384]{1,0:T(8,128)} %get-tuple-element.13, f32[1024]{0:T(1024)S(1)} %broadcast_maximum_fusion, s32[16384]{0:T(1024)S(1)} %fusion.10, s32[16384]{0:T(1024)S(1)} %bitcast.27, s32[1024]{0:T(1024)S(1)} %copy-done.1, s32[1024]{0:T(1024)S(1)} %copy-done.2), kind=kLoop, calls=%fused_computation.3 | loop fusion | flops 167770112 | bytes 67260416 | tf_op jit(solution)/shard_map/reduce_sum | solution.py:85
  214.0 9.7 %all_to_all.5 = f32[4,3,1024]{2,1,0:T(4,128)S(1)} all-to-all(f32[4,3,1024]{2,1,0:T(4,128)S(1)} %broadcast_in_dim.32), channel_id=1, replica_groups=mesh['blk_0'=4,'blk_1'=2,'blk_2'=8,'grp'=4] {'grp'}, dimensions={0} | all-to-all | bytes 98304 | tf_op jit(solution)/shard_map/all_to_all | solution.py:37
  223.9 0.6 fusion.12
  (20 shorter events, 0.4 us)
Async XLA Ops:
  6.5 142.3 %copy-start = (bf16[1024,256]{1,0:T(8,128)(2,1)S(1)}, bf16[1024,256]{1,0:T(8,128)(2,1)}, u32[]{:S(2)}) copy-start(bf16[1024,256]{1,0:T(8,128)(2,1)} %param.5) | copy-start | bytes 1572868
  6.5 35.9 %all-gather.7.cloned.1.call-start = ((), (), s32[]{:S(2)}) async-start(), calls=%async_computation.1 | async-start | bytes 1310720 | tf_op jit(solution)/shard_map/all_gather | solution.py:24
  13.7 127.6 %all-gather.9.cloned.1.call-start = ((), (), s32[]{:S(2)}) async-start(), calls=%async_computation.2 | async-start | bytes 9437184 | tf_op jit(solution)/shard_map/all_gather | solution.py:24
  148.8 28.2 %copy-start.1 = (s32[1024]{0:T(1024)S(1)}, s32[1024]{0:T(1024)}, u32[]{:S(2)}) copy-start(s32[1024]{0:T(1024)} %param.6) | copy-start | bytes 12292
  148.8 28.2 %copy-start.2 = (s32[1024]{0:T(1024)S(1)}, s32[1024]{0:T(1024)}, u32[]{:S(2)}) copy-start(s32[1024]{0:T(1024)} %param.7) | copy-start | bytes 12292
Sparse Core Ops, SparseCore 0:
  13.8 28.6 all-gather.6
  44.3 96.9 all-gather.8
where the time goes:
time: 232 us; the launch traced here: 231 us
  waiting for transfers between devices  93.2 us (40%)
  blocking collectives  51 us (22%)
  other arithmetic  37.6 us (16%)
  matrix products  28.2 us (12%)
  between operations  13.5 us (6%)
  local copies, waits for them, and re-layouts  7.94 us (3%)
    all_gather x2, waiting for transfers between devices, stacked_from(): parts = lax.all_gather(parts, axes[k], axis=0, tiled=True)  93.1 us
    all_gather x4, blocking collectives, stacked_from(): parts = lax.all_gather(parts, axes[k], axis=0, tiled=True)  41.3 us
    reduce_sum x1, other arithmetic, score_block(): totals = jnp.sum(weights, axis=1)  36.9 us
    dot_general x1, matrix products, score_block(): lax.dot_general(sources, block, (((1,), (1,)), ((), ())), preferred_eleme...  28.2 us
    all_to_all x1, blocking collectives, copy_for_each(): lax.all_to_all(jnp.broadcast_to(x[None], (size, *x.shape)), axis, 0, 0, t...  9.68 us
    transpose x1, local copies, waits for them, and re-layouts, stacked_from(): parts.transpose(*turned, *range(len(order), parts.ndim))  7.58 us
  transfers between devices with their start and end apart: 2, of which 2 were waited for; matrix products, arithmetic and copies ran while one was open for 0% of the time, Pallas kernels for 0%

commit v1 on v0

v1 whole, which is shorter than its diff:
```python
import jax
import jax.numpy as jnp
from jax import lax
from jax.experimental import pallas as pl
from jax.experimental.pallas import tpu as pltpu
from jax.sharding import Mesh
from jax.sharding import PartitionSpec as P

F32 = jnp.float32
BF16 = jnp.bfloat16
BLK = ("x", "yl", "z")
BLK_GRP = ("x", "yl", "z", "yh", "c")
NEG = -1e30
SCALE = 3.0
SCALE2 = SCALE * 1.4426950408889634
LN2 = 0.6931471805599453

OWN, Y, XP, XM, X2, YXP, YXM, YX2 = range(8)
ROW_DX = (0, 0, 1, 3, 2, 1, 3, 2)
ROW_DY = (0, 1, 0, 0, 0, 1, 1, 1)
COL_DZ = (0, 1, 7, 2, 6, 3, 5, 4)
META = 16
ROWS = 512
COLS = 256


def score(dots, part_ref, cc, src_part, relative, r, buf, top_of, tops, hits):
    sub = lax.broadcasted_iota(jnp.int32, (8, 128), 0).astype(F32)
    for k in range(ROWS // 128):
        lanes = slice(k * 128, (k + 1) * 128)
        own_part = jnp.broadcast_to(src_part[:, lanes], (8, 128))
        at = jnp.broadcast_to(relative[:, lanes], (8, 128)) - sub
        best = jnp.full((8, 128), NEG, F32)
        hit = hits[r, :, lanes]
        for t in range(COLS // 8):
            rows = slice(8 * t, 8 * t + 8)
            value = dots[rows, lanes]
            is_pos = at == float(8 * t)
            keep = (part_ref[cc, rows, :] != own_part) | is_pos
            masked = jnp.where(keep, value, NEG)
            hit = jnp.where(is_pos, value, hit)
            best = jnp.maximum(best, masked)
            buf[rows, lanes] = masked
        best = jnp.maximum(best, tops[r, :, lanes])
        tops[r, :, lanes] = best
        top_of[:, lanes] = best
        hits[r, :, lanes] = hit


def accumulate(r, buf, top_of, sum_tops, sums):
    for k in range(ROWS // 128):
        lanes = slice(k * 128, (k + 1) * 128)
        top = top_of[:, lanes]
        parts = [jnp.zeros((8, 128), F32), jnp.zeros((8, 128), F32)]
        for t in range(COLS // 8):
            parts[t % 2] = parts[t % 2] + jnp.exp2((buf[8 * t : 8 * t + 8, lanes] - top) * SCALE2)
        before = sum_tops[r, :, lanes]
        sums[r, :, lanes] = sums[r, :, lanes] * jnp.exp2((before - top) * SCALE2) + (parts[0] + parts[1])
        sum_tops[r, :, lanes] = top


def kernel(
    src_ref, pos_ref, spart_ref, dst_ref, dpart_ref, out_ref,
    rbuf, cbuf, part, buf_a, buf_b, top_a, top_b, tops, sum_tops, sums, hits, given, got,
    local_sem, send_sem, rrecv, crecv, precv, fsend, frecv,
):
    x, yl, z = lax.axis_index("x"), lax.axis_index("yl"), lax.axis_index("z")
    yh, c = lax.axis_index("yh"), lax.axis_index("c")
    nx, nz = lax.axis_size("x"), lax.axis_size("z")
    y = yh * 2 + yl
    ny = 4

    def ring(value, step, size):
        return lax.rem(value + step + size, size)

    y_next, y_prev = ring(y, 1, ny), ring(y, -1, ny)
    xp, xm = {"x": ring(x, 1, nx)}, {"x": ring(x, -1, nx)}
    zp, zm = {"z": ring(z, 1, nz)}, {"z": ring(z, -1, nz)}
    yp = {"yh": y_next // 2, "yl": lax.rem(y_next, 2)}
    ym = {"yh": y_prev // 2, "yl": lax.rem(y_prev, 2)}
    mate = {"c": 1 - c}

    load_rows = pltpu.make_async_copy(
        src_ref.at[pl.ds(pl.multiple_of(c * ROWS, ROWS), ROWS)], rbuf.at[OWN, pl.ds(META, ROWS)], local_sem.at[0]
    )
    load_cols = pltpu.make_async_copy(dst_ref, cbuf.at[0, pl.ds(META, COLS)], local_sem.at[1])
    load_rows.start()
    load_cols.start()

    barrier = pltpu.get_barrier_semaphore()
    greeted = [zp, zm]
    for dx in range(4):
        for dy in range(4):
            for dc in range(2):
                if dx or dy or dc:
                    there = ring(y, dy, ny)
                    greeted.append(
                        {"x": ring(x, dx, nx), "yh": there // 2, "yl": lax.rem(there, 2), "c": lax.rem(c + dc, 2)}
                    )
    for peer in greeted:
        pl.semaphore_signal(barrier, inc=1, device_id=peer, device_id_type=pl.DeviceIdType.MESH)

    own_pos = jnp.where(c == 0, pos_ref[0:2, :], pos_ref[2:4, :])
    own_part = jnp.where(c == 0, spart_ref[0:2, :], spart_ref[2:4, :])
    high = own_pos // 256
    meta = jnp.concatenate(
        [high.astype(F32), (own_pos - high * 256).astype(F32), own_part.astype(F32), jnp.zeros((10, 256), F32)], axis=0
    )
    rbuf[OWN, 0:META, :] = meta.astype(BF16)
    cbuf[0, 0:META, :] = jnp.broadcast_to(dpart_ref[...].astype(F32), (META, 256)).astype(BF16)
    tops[...] = jnp.full(tops.shape, NEG, F32)
    sum_tops[...] = jnp.full(tops.shape, NEG, F32)
    sums[...] = jnp.zeros(tops.shape, F32)
    hits[...] = jnp.zeros(tops.shape, F32)

    load_rows.wait()
    load_cols.wait()
    pl.semaphore_wait(barrier, len(greeted))

    sent = []

    def send(src, dst, sem, peer):
        copy = pltpu.make_async_remote_copy(
            src_ref=src, dst_ref=dst, send_sem=send_sem.at[len(sent)], recv_sem=sem,
            device_id=peer, device_id_type=pl.DeviceIdType.MESH,
        )
        copy.start()
        sent.append(copy)

    def arrived(ref, sem):
        pltpu.make_async_remote_copy(
            src_ref=ref, dst_ref=ref, send_sem=send_sem.at[0], recv_sem=sem,
            device_id=mate, device_id_type=pl.DeviceIdType.MESH,
        ).wait_recv()

    def row_chunk(slot, chunk):
        return rbuf.at[slot, pl.ds(272 * chunk, 272 - 16 * chunk)]

    def send_rows(slot, chunk, to, peer):
        send(row_chunk(slot, chunk), row_chunk(to, chunk), rrecv.at[to, chunk], peer)

    def rows_arrived(slot, chunk):
        arrived(row_chunk(slot, chunk), rrecv.at[slot, chunk])

    def col_chunk(d, chunk):
        return cbuf.at[2 * d, pl.ds(144 * chunk, 144 - 16 * chunk)]

    def send_cols(d, chunk, to, peer):
        send(col_chunk(d, chunk), col_chunk(to, chunk), crecv.at[to, chunk], peer)

    def cols_arrived(d, chunk):
        arrived(col_chunk(d, chunk), crecv.at[d, chunk])

    def share(d):
        send(cbuf.at[2 * d], cbuf.at[2 * d + 1], precv.at[d], mate)

    def spread_part(cc):
        line = cbuf[cc, 0:META, :].astype(F32)[0:1, :]
        for k in range(2):
            part[cc, 128 * k : 128 * k + 128, :] = jnp.broadcast_to(line[:, 128 * k : 128 * k + 128], (128, 128)).T

    def shared_arrived(d):
        arrived(cbuf.at[2 * d + 1], precv.at[d])
        spread_part(2 * d + 1)

    def first(r, cc, buf, top_of):
        d = cc // 2
        step = lax.div(d + 1, 2)
        dz = jnp.where(lax.rem(d, 2) == 1, step, nz - step)
        core = jnp.where(lax.rem(cc, 2) == 0, c, 1 - c)
        blk = (x * 2 + yl) * nz + lax.rem(z + dz, nz)
        base = ((blk * 2 + yh) * 2 + core) * COLS
        line = rbuf[r, 0:META, :].astype(F32)
        src_part = jnp.concatenate([line[4:5], line[5:6]], axis=1)
        positive = jnp.concatenate([line[0:1], line[1:2]], axis=1) * 256.0
        positive = positive + jnp.concatenate([line[2:3], line[3:4]], axis=1)
        dots = lax.dot_general(
            cbuf[cc, META : META + COLS, :], rbuf[r, META : META + ROWS, :],
            (((1,), (1,)), ((), ())), preferred_element_type=F32,
        )
        score(dots, part, cc, src_part, positive - base.astype(F32), r, buf, top_of, tops, hits)

    def tiles(r0, r1, c0, c1, stride=1):
        width = -(-(c1 - c0) // stride)
        count = (r1 - r0) * width

        def where(i):
            return r0 + lax.div(i, width), c0 + stride * lax.rem(i, width)

        def one(i, buf, top_of):
            first(*where(i), buf, top_of)

        def two(i, buf, top_of):
            accumulate(where(i)[0], buf, top_of, sum_tops, sums)

        assert count % 2 == 0 or count == 1
        if count == 1:
            one(jnp.int32(0), buf_a, top_a)
            two(jnp.int32(0), buf_a, top_a)
            return
        one(jnp.int32(0), buf_a, top_a)

        def pair(j, carry):
            i = 2 * j
            one(i + 1, buf_b, top_b)
            two(i, buf_a, top_a)
            one(i + 2, buf_a, top_a)
            two(i + 1, buf_b, top_b)
            return carry

        lax.fori_loop(0, count // 2 - 1, pair, 0)
        one(jnp.int32(count - 1), buf_b, top_b)
        two(jnp.int32(count - 2), buf_a, top_a)
        two(jnp.int32(count - 1), buf_b, top_b)

    finals = []

    def finish(r):
        sub = lax.broadcasted_iota(jnp.int32, (8, ROWS), 0)
        top = jnp.max(tops[r], axis=0, keepdims=True)
        total = jnp.sum(sums[r] * jnp.exp2((sum_tops[r] - top) * SCALE2), axis=0, keepdims=True)
        hit = jnp.sum(hits[r], axis=0, keepdims=True)
        line = jnp.where(sub == 0, top, jnp.where(sub == 1, total, hit))
        here = x * ny + y
        if r == OWN:
            got[c, here] = line
        given[r] = line
        bx, by = ring(x, ROW_DX[r], nx), lax.rem(yl + ROW_DY[r], 2)
        for other_yh in (0, 1):
            for other_c in (0, 1):
                if r == OWN and other_yh == 0 and other_c == 0:
                    continue
                if r == OWN:
                    peer = {"yh": lax.rem(yh + other_yh, 2), "c": lax.rem(c + other_c, 2)}
                else:
                    peer = {"x": bx, "yl": by, "yh": other_yh, "c": other_c}
                copy = pltpu.make_async_remote_copy(
                    src_ref=given.at[r], dst_ref=got.at[c, here], send_sem=fsend.at[len(finals)],
                    recv_sem=frecv.at[c, here], device_id=peer, device_id_type=pl.DeviceIdType.MESH,
                )
                copy.start()
                finals.append(copy)

    for chunk in (0, 1):
        send_cols(0, chunk, 1, zm)
        send_cols(0, 1 - chunk, 2, zp)
        send_rows(OWN, chunk, XP, xm)
        send_rows(OWN, 1 - chunk, XM, xp)
        send_rows(OWN, chunk, Y, (yp, ym)[chunk])
    share(0)
    spread_part(0)
    tiles(0, 1, 0, 1)
    shared_arrived(0)
    tiles(0, 1, 1, 2)

    cols_arrived(1, 0)
    send_cols(1, 0, 3, zm)
    cols_arrived(2, 1)
    send_cols(2, 1, 4, zp)
    rows_arrived(XP, 0)
    send_rows(XP, 0, X2, xm)
    send_rows(XP, 0, YXP, yp)
    rows_arrived(XM, 1)
    send_rows(XM, 1, X2, xp)
    send_rows(XM, 1, YXM, ym)
    cols_arrived(1, 1)
    send_cols(1, 1, 3, zm)
    share(1)
    cols_arrived(2, 0)
    send_cols(2, 0, 4, zp)
    share(2)
    spread_part(2)
    spread_part(4)
    rows_arrived(Y, 0)
    rows_arrived(Y, 1)
    tiles(1, 2, 0, 2)
    tiles(0, 2, 2, 6, 2)
    shared_arrived(1)
    shared_arrived(2)
    tiles(0, 2, 3, 6, 2)

    cols_arrived(3, 0)
    send_cols(3, 0, 5, zm)
    cols_arrived(4, 1)
    send_cols(4, 1, 6, zp)
    rows_arrived(XP, 1)
    send_rows(XP, 1, YXP, ym)
    rows_arrived(XM, 0)
    send_rows(XM, 0, YXM, yp)
    cols_arrived(3, 1)
    send_cols(3, 1, 5, zm)
    share(3)
    cols_arrived(4, 0)
    send_cols(4, 0, 6, zp)
    share(4)
    tiles(2, 4, 0, 6)

    cols_arrived(5, 0)
    send_cols(5, 0, 7, zm)
    cols_arrived(6, 1)
    send_cols(6, 1, 7, zp)
    rows_arrived(X2, 0)
    send_rows(X2, 0, YX2, yp)
    rows_arrived(X2, 1)
    send_rows(X2, 1, YX2, ym)
    spread_part(6)
    spread_part(8)
    shared_arrived(3)
    shared_arrived(4)
    tiles(0, 4, 6, 10)

    cols_arrived(5, 1)
    share(5)
    cols_arrived(6, 0)
    share(6)
    tiles(4, 5, 0, 10)
    spread_part(10)
    spread_part(12)
    shared_arrived(5)
    shared_arrived(6)
    cols_arrived(7, 0)
    cols_arrived(7, 1)
    share(7)
    tiles(0, 5, 10, 14)
    spread_part(14)
    shared_arrived(7)
    tiles(0, 5, 14, 16)
    for r in range(5):
        finish(r)
    rows_arrived(YXP, 0)
    rows_arrived(YXP, 1)
    tiles(5, 6, 0, 16)
    finish(5)
    rows_arrived(YXM, 0)
    rows_arrived(YXM, 1)
    tiles(6, 7, 0, 16)
    finish(6)
    rows_arrived(YX2, 0)
    rows_arrived(YX2, 1)
    tiles(7, 8, 0, 16)
    finish(7)

    for copy in sent:
        copy.wait_send()
    for r, copy in enumerate(finals):
        copy.wait_send()
    for half in (0, 1):
        for dx in range(4):
            for dy in range(4):
                for_own = dx == 0 and dy == 0
                whose = ring(x, dx, nx) * ny + ring(y, dy, ny)
                core = lax.rem(c + half, 2)
                if not (for_own and half == 0):
                    arrived(got.at[core, whose], frecv.at[core, whose])
    for half in (0, 1):
        every = got[half]
        tops_of = every[:, 0, :]
        top = jnp.max(tops_of, axis=0, keepdims=True)
        total = jnp.sum(every[:, 1, :] * jnp.exp2((tops_of - top) * SCALE2), axis=0, keepdims=True)
        hit = jnp.sum(every[:, 2, :], axis=0, keepdims=True)
        out_ref[half : half + 1, :] = SCALE * (top - hit) + jnp.log(total)


def on_device(sources, positive, src_part, destinations, dst_part):
    vmem, anywhere = pl.BlockSpec(memory_space=pltpu.VMEM), pl.BlockSpec(memory_space=pl.ANY)
    out = pl.pallas_call(
        kernel,
        out_shape=jax.ShapeDtypeStruct((2, ROWS), F32),
        in_specs=[anywhere, vmem, vmem, anywhere, vmem],
        out_specs=vmem,
        scratch_shapes=[
            pltpu.VMEM((8, META + ROWS, 256), BF16),
            pltpu.VMEM((16, META + COLS, 256), BF16),
            pltpu.VMEM((16, COLS, 128), F32),
            pltpu.VMEM((COLS, ROWS), F32),
            pltpu.VMEM((COLS, ROWS), F32),
            pltpu.VMEM((8, ROWS), F32),
            pltpu.VMEM((8, ROWS), F32),
            pltpu.VMEM((8, 8, ROWS), F32),
            pltpu.VMEM((8, 8, ROWS), F32),
            pltpu.VMEM((8, 8, ROWS), F32),
            pltpu.VMEM((8, 8, ROWS), F32),
            pltpu.VMEM((8, 8, ROWS), F32),
            pltpu.VMEM((2, 16, 8, ROWS), F32),
            pltpu.SemaphoreType.DMA((2,)),
            pltpu.SemaphoreType.DMA((40,)),
            pltpu.SemaphoreType.DMA((8, 2)),
            pltpu.SemaphoreType.DMA((8, 2)),
            pltpu.SemaphoreType.DMA((8,)),
            pltpu.SemaphoreType.DMA((31,)),
            pltpu.SemaphoreType.DMA((2, 16)),
        ],
        compiler_params=pltpu.CompilerParams(
            collective_id=0, has_side_effects=True, vmem_limit_bytes=48 * 1024 * 1024
        ),
        name="loss",
    )(
        sources,
        positive.reshape(4, 256),
        src_part.reshape(4, 256),
        destinations,
        dst_part.reshape(1, 256),
    )
    return out.reshape(-1)


def solution(mesh):
    finer = Mesh(mesh.devices.reshape(4, 2, 8, 2, 2), ("x", "yl", "z", "yh", "c"))
    placed = (P(BLK, None), P(BLK), P(BLK), P(BLK_GRP, None), P(BLK_GRP))
    return jax.shard_map(on_device, mesh=finer, in_specs=placed, out_specs=P(BLK), check_vma=False)
```

time: 232 us -> 63.4 us (0.27)
  waiting for transfers between devices: 93.2 us -> 0 us
  Pallas kernels: 0 us -> 59.2 us
  blocking collectives: 51 us -> 0 us
  other arithmetic: 37.6 us -> 0 us
  matrix products: 28.2 us -> 0 us
  between operations: 13.5 us -> 0.01 us
  local copies, waits for them, and re-layouts: 7.94 us -> 3.93 us
    all_gather x2 -> x0, waiting for transfers between devices: 93.1 us -> none  [stacked_from(): parts = lax.all_gather(parts, axes[k], axis=0, tiled=True)]
    pallas_call x0 -> x1, Pallas kernels: none -> 59.2 us  [on_device(): pl.pallas_call(kernel, out_shape=jax.ShapeDtypeStruct((2, ROWS), F32), in...]
    all_gather x4 -> x0, blocking collectives: 41.3 us -> none  [stacked_from(): parts = lax.all_gather(parts, axes[k], axis=0, tiled=True)]
    reduce_sum x1 -> x0, other arithmetic: 36.9 us -> none  [score_block(): totals = jnp.sum(weights, axis=1)]
    dot_general x1 -> x0, matrix products: 28.2 us -> none  [score_block(): lax.dot_general(sources, block, (((1,), (1,)), ((), ())), preferred_eleme...]
    all_to_all x1 -> x0, blocking collectives: 9.68 us -> none  [copy_for_each(): lax.all_to_all(jnp.broadcast_to(x[None], (size, *x.shape)), axis, 0, 0, t...]
    transpose x1 -> x0, local copies, waits for them, and re-layouts: 7.58 us -> none  [stacked_from(): parts.transpose(*turned, *range(len(order), parts.ndim))]
    unnamed x10 -> x9, local copies, waits for them, and re-layouts: 0.06 us -> 3.21 us
  transfers between devices with their start and end apart: 2 -> 0, of which waited for: 2 -> 0; matrix products, arithmetic and copies ran while one was open for 0% -> 0% of each run, Pallas kernels for 0% -> 0%
where the time goes in v1:
time: 63.4 us; the launch traced here: 63.2 us
  Pallas kernels  59.2 us (93%)
  local copies, waits for them, and re-layouts  3.93 us (6%)
    pallas_call x1, Pallas kernels, on_device(): pl.pallas_call(kernel, out_shape=jax.ShapeDtypeStruct((2, ROWS), F32), in...  59.2 us
    unnamed x9, local copies, waits for them, and re-layouts  3.21 us

profile of v1, /device:TPU:1, one launch (start us, length us, event | category | flops | bytes accessed | tf_op | source)
XLA Modules:
  0.0 63.2 jit_solution(6568912297980337689)
XLA Ops:
  0.0 0.0 copy-start.3
  0.0 0.7 %reshape.12.pos_ref = s32[4,256]{1,0:T(4,128)S(1)} reshape(s32[1024]{0:T(1024)} %param.6) | data formatting | bytes 8192 | tf_op jit(solution)/shard_map/reshape | solution.py:399
  0.7 0.0 copy-done.3
  0.7 0.0 copy-start.2
  0.7 0.7 %copy-done.2 = s32[256]{0:T(256)S(1)} copy-done((s32[256]{0:T(256)S(1)}, s32[256]{0:T(256)}, u32[]{:S(2)}) %copy-start.2) | copy-done | bytes 1048
  1.4 0.0 copy-start
  1.4 1.0 %copy-done = bf16[1024,256]{1,0:T(8,128)(2,1)S(1)} copy-done((bf16[1024,256]{1,0:T(8,128)(2,1)S(1)}, bf16[1024,256]{1,0:T(8,128)(2,1)}, u32[]{:S(2)}) %copy-start) | copy-done | bytes 524312
  2.4 0.0 copy-start.1
  2.4 0.9 %copy-done.1 = bf16[256,256]{1,0:T(8,128)(2,1)S(1)} copy-done((bf16[256,256]{1,0:T(8,128)(2,1)S(1)}, bf16[256,256]{1,0:T(8,128)(2,1)}, u32[]{:S(2)}) %copy-start.1) | copy-done | bytes 131096
  3.3 59.2 %loss.1 = f32[2,512]{1,0:T(2,128)S(1)} custom-call(bf16[1024,256]{1,0:T(8,128)(2,1)S(1)} %copy-done, s32[4,256]{1,0:T(4,128)S(1)} %reshape.12.pos_ref, s32[4,256]{1,0:T(4,128)S(1)} %reshape.13.spart_ref, bf16[256,256]{1,0:T(8,128)(2,1)S(1)} %copy-done.1, s32[1,256]{1,0:T(1,128)S(1)} %bitcast.4), custom_call_target="tpu_custom_call" | custom-call | tf_op jit(solution)/shard_map/loss/pallas_call | solution.py:366
  62.6 0.6 copy.6
  (1 shorter events, 0.0 us)
Async XLA Ops:
  0.0 0.7 %copy-start.3 = (s32[1024]{0:T(1024)S(1)}, s32[1024]{0:T(1024)}, u32[]{:S(2)}) copy-start(s32[1024]{0:T(1024)} %param.7) | copy-start | bytes 12292
  0.7 0.7 %copy-start.2 = (s32[256]{0:T(256)S(1)}, s32[256]{0:T(256)}, u32[]{:S(2)}) copy-start(s32[256]{0:T(256)} %param.9) | copy-start | bytes 3076
  1.4 1.0 %copy-start = (bf16[1024,256]{1,0:T(8,128)(2,1)S(1)}, bf16[1024,256]{1,0:T(8,128)(2,1)}, u32[]{:S(2)}) copy-start(bf16[1024,256]{1,0:T(8,128)(2,1)} %src_ref.1) | copy-start | bytes 1572868
  2.4 0.9 %copy-start.1 = (bf16[256,256]{1,0:T(8,128)(2,1)S(1)}, bf16[256,256]{1,0:T(8,128)(2,1)}, u32[]{:S(2)}) copy-start(bf16[256,256]{1,0:T(8,128)(2,1)} %dst_ref.1) | copy-start | bytes 393220
